TPU v7x, 32 devices: a whole 2x2x4 slice. The times are simulated.
32 devices in a mesh: frag: 2 (over x), dev2: 4 (over z), dev: 4 (over y, core).
Axes of the slice: x: 2, y: 2, z: 4, core: 2. Of those that a mesh axis runs over, the one named last changes fastest.
Arguments:
- ao_ints: bfloat16 [256, 128, 128, 128], P(('frag', 'dev'), 'dev2'), parts along dimension 0
- c_occ: bfloat16 [256, 24], P('frag'), parts along dimension 0
- c_virt: bfloat16 [256, 80], P('frag'), parts along dimension 0
Outputs:
- output: float32 [48, 80, 1920], P('frag', None, ('dev2', 'dev')), parts along dimension 0
There are 2 independent parts. A program takes and returns all parts, laid end to end along the dimension named above; each array names one.
All inputs are finite; a program needn't handle non-finite values.
Results may differ from a plain program's by a relative error of at most 0.001.
Values are sent between devices in bfloat16 or wider.
A program may use at most 1 GiB of HBM per device.

v0:
```python
import jax
import jax.numpy as jnp
from jax import lax
from jax.sharding import PartitionSpec as P


def solution(mesh):
    def local_block(ao_blk, c_occ, c_virt):
        occ_num = c_occ.shape[1]
        virt_num = c_virt.shape[1]
        t_one = jnp.einsum("pqrs,rj->pqsj", ao_blk, c_occ, preferred_element_type=jnp.float32).astype(jnp.bfloat16)
        half_blk = jnp.einsum("pqsj,sb->pqjb", t_one, c_virt, preferred_element_type=jnp.float32).astype(jnp.bfloat16)
        half_blk = half_blk.reshape(ao_blk.shape[0], ao_blk.shape[1], occ_num * virt_num)
        q_whole = lax.all_to_all(half_blk, "dev2", 2, 1, tiled=True)
        pq_whole = lax.all_to_all(q_whole, "dev", 2, 0, tiled=True)
        e_part = jnp.einsum("pi,pqk->iqk", c_occ, pq_whole, preferred_element_type=jnp.float32)
        return jnp.einsum("iqk,qa->iak", e_part, c_virt.astype(jnp.float32), precision=lax.Precision.HIGHEST, preferred_element_type=jnp.float32)

    return jax.shard_map(
        local_block, mesh=mesh,
        in_specs=(P(("frag", "dev"), "dev2", None, None), P("frag", None), P("frag", None)),
        out_specs=P("frag", None, ("dev2", "dev")),
        check_vma=False)
```

profile of v0, /device:TPU:0, one launch (start us, length us, event | category | flops | bytes accessed | tf_op | source)
XLA Modules:
  0.0 242.1 jit_solution(10055565203633734289)
XLA Ops:
  0.0 0.0 copy-start
  0.0 0.7 copy-done
  0.7 16.2 %fusion.6 = bf16[32,32,24,80]{3,2,1,0:T(8,128)(2,1)} fusion(bf16[32,32,128,128]{3,2,1,0:T(8,128)(2,1)} %param.3, bf16[128,80]{0,1:T(8,128)(2,1)S(1)} %copy-done, bf16[128,24]{0,1:T(8,128)(2,1)} %param.4), kind=kOutput, calls=%fused_computation.5 | convolution fusion | flops 1313734656 | bytes 37513216 | tf_op jit(solution)/shard_map/pqsj,sb->pqjb/dot_general | solution.py:12
  16.9 15.7 %copy.21 = bf16[32,32,24,80]{1,0,3,2:T(8,128)(2,1)} copy(bf16[32,32,24,80]{3,2,1,0:T(8,128)(2,1)} %fusion.6) | data formatting | bytes 7864320 | tf_op jit(solution)/shard_map/reshape | solution.py:13
  32.6 18.1 %reshape.8 = bf16[4,2,245760]{2,1,0:T(2,128)(2,1)} reshape(bf16[1920,32,32]{2,1,0:T(8,128)(2,1)} %bitcast.33) | data formatting | bytes 7864320
  50.8 94.6 %all_to_all.36 = bf16[4,2,245760]{2,1,0:T(2,128)(2,1)} all-to-all(bf16[4,2,245760]{2,1,0:T(2,128)(2,1)} %reshape.8), channel_id=1, replica_groups=mesh['frag'=2,'dev2'=4,'dev'=4] {'dev2'}, dimensions={0} | all-to-all | bytes 7864320 | tf_op jit(solution)/shard_map/all_to_all | solution.py:14
  145.3 11.5 %reshape.9 = bf16[1920,32,32]{2,1,0:T(8,128)(2,1)} reshape(bf16[4,2,245760]{2,1,0:T(2,128)(2,1)} %all_to_all.36) | data formatting | bytes 7864320
  156.8 18.5 %copy.22 = bf16[32,32,4,480]{3,2,1,0:T(4,128)(2,1)} copy(bf16[32,32,4,480]{1,0,3,2:T(8,128)(2,1)} %bitcast.32) | data formatting | bytes 7864320 | tf_op jit(solution)/shard_map/all_to_all | solution.py:14
  175.3 5.5 %copy.13 = bf16[32,4,32,480]{3,2,1,0:T(8,128)(2,1)} copy(bf16[32,4,32,480]{3,1,2,0:T(4,128)(2,1)} %bitcast.34) | data formatting | bytes 7864320 | tf_op jit(solution)/shard_map/all_to_all | solution.py:14
  180.7 7.9 %copy.14 = bf16[32,128,480]{1,0,2:T(8,128)(2,1)} copy(bf16[32,128,480]{2,1,0:T(8,128)(2,1)} %bitcast.35) | data formatting | bytes 7864320 | tf_op jit(solution)/shard_map/all_to_all | solution.py:14
  188.6 48.9 %all_to_all.37 = bf16[32,128,480]{1,0,2:T(8,128)(2,1)S(1)} all-to-all(bf16[32,128,480]{1,0,2:T(8,128)(2,1)} %copy.14), channel_id=1, replica_groups=mesh['frag'=2,'dev2'=4,'dev'=4] {'dev'}, dimensions={2} | all-to-all | bytes 7864320 | tf_op jit(solution)/shard_map/all_to_all | solution.py:15
  237.5 0.0 copy-start.1
  237.5 1.5 copy.16
  239.0 0.0 copy-done.1
  239.0 0.6 fusion.11
  239.6 2.5 %fusion.14 = f32[24,80,120]{2,1,0:T(8,128)} fusion(f32[24,128,120]{1,0,2:T(8,128)S(1)} %fusion.11, bf16[128,80]{0,1:T(8,128)(2,1)S(1)} %copy-done), kind=kOutput, calls=%fused_computation.9 | convolution fusion | flops 353894400 | bytes 2416640 | tf_op jit(solution)/shard_map/iqk,qa->iak/dot_general | solution.py:17
Async XLA Ops:
  0.0 0.7 copy-start
  237.5 1.5 copy-start.1
where the time goes:
time: 243 us; the launch traced here: 242 us
  blocking collectives  143 us (59%)
  local copies, waits for them, and re-layouts  79.4 us (33%)
  matrix products  19.3 us (8%)
    all_to_all x1, blocking collectives, local_block(): q_whole = lax.all_to_all(half_blk, 'dev2', 2, 1, tiled=True)  94.6 us
    all_to_all x1, blocking collectives, local_block(): pq_whole = lax.all_to_all(q_whole, 'dev', 2, 0, tiled=True)  48.9 us
    all_to_all x3, local copies, waits for them, and re-layouts, local_block(): q_whole = lax.all_to_all(half_blk, 'dev2', 2, 1, tiled=True)  31.8 us
    unnamed x6, local copies, waits for them, and re-layouts  30.3 us
    dot_general x1, matrix products, local_block(): jnp.einsum('pqsj,sb->pqjb', t_one, c_virt, preferred_element_type=jnp.flo...  16.2 us
    reshape x1, local copies, waits for them, and re-layouts, local_block(): half_blk.reshape(ao_blk.shape[0], ao_blk.shape[1], occ_num * virt_num)  15.7 us

commit v1 on v0

v1 whole, which is shorter than its diff:
```python
import functools

import jax
import jax.numpy as jnp
from jax import lax
from jax.experimental import pallas as pl
from jax.experimental.pallas import tpu as pltpu
from jax.sharding import PartitionSpec as P

MESH = pl.DeviceIdType.MESH
F32 = jnp.float32
BF16 = jnp.bfloat16
OCC = 24
VIRT = 80
LANES = 120
QSUB = 2
QBLK = 8
STEPS = 32 // QSUB
BLKS = 32 // QBLK
SUBS = QBLK // QSUB
AHEAD = 4


def dot(a, b):
    return jnp.dot(a, b, preferred_element_type=F32)


def dot_nt(a, b):
    return lax.dot_general(a, b, (((1,), (1,)), ((), ())), preferred_element_type=F32)


def iota(shape, dim):
    return lax.broadcasted_iota(jnp.int32, shape, dim)


def select(mask):
    return jnp.where(mask, 1.0, 0.0).astype(BF16)


def kernel(ao_ref, occ_ref, virt_ref, out_ref,
           a_buf, occ_lhs, virt_rhs, kron_own, kron_sib, virt_t,
           h_buf, h_in, e_buf, y_in, e_all,
           a_sem, hs_sem, hr_sem, ys_sem, yr_sem, zs_sem, zr_sem):
    z = lax.axis_index("dev2")
    dev = lax.axis_index("dev")
    y = dev // 2
    core = dev % 2
    sib = y * 2 + (1 - core)
    across = (1 - y) * 2 + core
    half = z // 2
    order = (3 * (1 - half), 2 - half, 1 - z + 4 * half)

    def a_copy(s):
        return pltpu.make_async_copy(
            ao_ref.at[:, pl.ds(s * QSUB, QSUB)], a_buf.at[s], a_sem.at[s])

    def h_copy(s):
        return pltpu.make_async_remote_copy(
            src_ref=h_buf.at[1 - core, pl.ds(s * QSUB, QSUB)],
            dst_ref=h_in.at[pl.ds(s * QSUB, QSUB)],
            send_sem=hs_sem.at[s], recv_sem=hr_sem.at[s],
            device_id={"dev": sib}, device_id_type=MESH)

    def y_copy(blk, zz):
        rows = pl.ds(zz * (OCC * QBLK), OCC * QBLK)
        return pltpu.make_async_remote_copy(
            src_ref=e_buf.at[1 - y, blk, rows], dst_ref=y_in.at[blk, rows],
            send_sem=ys_sem.at[blk, zz], recv_sem=yr_sem.at[blk, zz],
            device_id={"dev": across}, device_id_type=MESH)

    def z_copy(blk, zz, src):
        rows = pl.ds(zz * (OCC * QBLK), OCC * QBLK)
        return pltpu.make_async_remote_copy(
            src_ref=e_buf.at[y, blk, rows], dst_ref=e_all.at[src * BLKS + blk],
            send_sem=zs_sem.at[blk, zz], recv_sem=zr_sem.at[blk, src],
            device_id={"dev2": zz}, device_id_type=MESH)

    barrier = pltpu.get_barrier_semaphore()
    for peer in ({"dev": sib}, {"dev": across}, {"dev2": (z + 1) % 4}, {"dev2": (z + 2) % 4}, {"dev2": (z + 3) % 4}):
        pl.semaphore_signal(barrier, inc=1, device_id=peer, device_id_type=MESH)

    for s in range(AHEAD):
        a_copy(s).start()

    occ = occ_ref[...]
    row = iota((OCC, OCC), 0)
    perm = select(iota((OCC, OCC), 1) == 3 * (row % 8) + row // 8)
    occ_t = dot_nt(perm, occ).astype(BF16)
    zero = jnp.zeros((OCC, 128), BF16)
    occ_lhs[...] = jnp.concatenate(
        [jnp.concatenate([occ_t, zero], 1), jnp.concatenate([zero, occ_t], 1)], 0)
    virt = virt_ref[...]
    col = iota((VIRT, 256), 1)
    lane = col % 128
    pair = (col // 128) * LANES + lane
    for jj in range(3):
        pick = select((pair == jj * VIRT + iota((VIRT, 256), 0)) & (lane < LANES))
        virt_rhs[pl.ds(jj * 128, 128), :] = dot(virt, pick).astype(BF16)
    row = iota((192, OCC), 0)
    pick_i = select(row % OCC == iota((192, OCC), 1))
    pick_p = select(iota((32, 256), 1) // 8 == iota((32, 256), 0))
    row = iota((192, 256), 0)
    keep = iota((192, 256), 1) % 8 == 2 * ((row % 96) // OCC) + row // 96
    for dst, who in ((kron_own, dev), (kron_sib, sib)):
        part = dot_nt(pick_i, occ_ref[pl.ds(pl.multiple_of(who * 32, 32), 32), :]).astype(BF16)
        dst[...] = jnp.where(keep, dot(part, pick_p), 0.0).astype(BF16)
    eye = select(iota((VIRT, VIRT), 0) == iota((VIRT, VIRT), 1))
    virt_t[...] = dot_nt(eye, virt).astype(BF16)

    pl.semaphore_wait(barrier, 5)

    def half_step(s):
        for qq in range(QSUB):
            rows = []
            for p in range(0, 32, 4):
                a = [a_buf[s, p + k, qq] for k in range(4)]
                w = jnp.concatenate(
                    [jnp.concatenate(a[:2], 1), jnp.concatenate(a[2:], 1)], 0)
                r = dot(occ_lhs[...], w)
                for k in range(4):
                    part = r[(k // 2) * OCC:(k // 2 + 1) * OCC, (k % 2) * 128:(k % 2 + 1) * 128]
                    rows.append(jnp.concatenate([part[0:8], part[8:16], part[16:24]], 1))
            t_one = jnp.concatenate(rows, 0).astype(BF16)
            h = dot(t_one, virt_rhs[...]).astype(BF16)
            h_buf[0, s * QSUB + qq] = h[:, :128]
            h_buf[1, s * QSUB + qq] = h[:, 128:]

    def e_step(s):
        q = s * QSUB
        own = jnp.concatenate([h_buf[core, q + k] for k in range(QSUB)], 1)
        other = jnp.concatenate([h_in[q + k] for k in range(QSUB)], 1)
        e = dot(kron_own[...], own) + dot(kron_sib[...], other)
        blk = s // SUBS
        for k in range(QSUB):
            for yy in range(2):
                e_buf[yy, blk, pl.ds((s % SUBS) * QSUB + k, 96, stride=QBLK), :] = (
                    e[yy * 96:(yy + 1) * 96, k * 128:(k + 1) * 128])

    def step(s, carry):
        @pl.when(s < STEPS)
        def _():
            a_copy(s).wait()

            @pl.when(s + AHEAD < STEPS)
            def _():
                a_copy(s + AHEAD).start()
            half_step(s)
            h_copy(s).start()

        @pl.when(s > 0)
        def _():
            h_copy(s - 1).wait_recv()
            e_step(s - 1)

            @pl.when((s - 1) % SUBS == SUBS - 1)
            def _():
                for zz in (*order, z):
                    y_copy((s - 1) // SUBS, zz).start()
        return carry

    lax.fori_loop(0, STEPS + 1, step, 0)

    def sum_step(blk, carry):
        for zz in order:
            rows = pl.ds(pl.multiple_of(zz * (OCC * QBLK), 8), OCC * QBLK)
            y_copy(blk, zz).wait_recv()
            e_buf[y, blk, rows] = e_buf[y, blk, rows] + y_in[blk, rows]
            z_copy(blk, zz, z).start()
        rows = pl.ds(pl.multiple_of(z * (OCC * QBLK), 8), OCC * QBLK)
        y_copy(blk, z).wait_recv()
        e_all[z * BLKS + blk] = e_buf[y, blk, rows] + y_in[blk, rows]
        return carry

    lax.fori_loop(0, BLKS, sum_step, 0)

    def arrived(blk, carry):
        for d in range(1, 4):
            z_copy(blk, z, (z + d) % 4).wait_recv()
        return carry

    lax.fori_loop(0, BLKS, arrived, 0)

    def v_step(n, carry):
        for pr in range(2):
            parts = []
            for k in range(2):
                i = n * 4 + pr * 2 + k
                e = e_all[:, pl.ds(pl.multiple_of(i * QBLK, 8), QBLK), :].reshape(128, 128)
                hi = e.astype(BF16)
                rest = e - hi.astype(F32)
                mid = rest.astype(BF16)
                low = (rest - mid.astype(F32)).astype(BF16)
                parts.append((hi, mid, low))
            v = jnp.zeros((VIRT, 256), F32)
            for a, b in zip(*parts):
                v = v + dot(virt_t[...], jnp.concatenate([a, b], 1))
            for k in range(2):
                out_ref[n * 4 + pr * 2 + k] = v[:, k * 128:k * 128 + LANES]
        return carry

    lax.fori_loop(0, OCC // 4, v_step, 0)

    def sent(s, carry):
        h_copy(s).wait_send()
        return carry

    lax.fori_loop(0, STEPS, sent, 0)

    def sent_blk(blk, carry):
        for zz in (*order, z):
            y_copy(blk, zz).wait_send()
        for zz in order:
            z_copy(blk, zz, z).wait_send()
        return carry

    lax.fori_loop(0, BLKS, sent_blk, 0)


def solution(mesh):
    def local_block(ao_blk, c_occ, c_virt):
        vmem = pl.BlockSpec(memory_space=pltpu.VMEM)
        return pl.pallas_call(
            kernel,
            out_shape=jax.ShapeDtypeStruct((OCC, VIRT, LANES), F32),
            in_specs=[pl.BlockSpec(memory_space=pl.ANY), vmem, vmem],
            out_specs=vmem,
            scratch_shapes=[
                pltpu.VMEM((STEPS, 32, QSUB, 128, 128), BF16),
                pltpu.VMEM((2 * OCC, 256), BF16),
                pltpu.VMEM((384, 256), BF16),
                pltpu.VMEM((192, 256), BF16),
                pltpu.VMEM((192, 256), BF16),
                pltpu.VMEM((VIRT, 128), BF16),
                pltpu.VMEM((2, 32, 256, 128), BF16),
                pltpu.VMEM((32, 256, 128), BF16),
                pltpu.VMEM((2, BLKS, 4 * OCC * QBLK, 128), F32),
                pltpu.VMEM((BLKS, 4 * OCC * QBLK, 128), F32),
                pltpu.VMEM((4 * BLKS, OCC * QBLK, 128), F32),
                pltpu.SemaphoreType.DMA((STEPS,)),
                pltpu.SemaphoreType.DMA((STEPS,)),
                pltpu.SemaphoreType.DMA((STEPS,)),
                pltpu.SemaphoreType.DMA((BLKS, 4)),
                pltpu.SemaphoreType.DMA((BLKS, 4)),
                pltpu.SemaphoreType.DMA((BLKS, 4)),
                pltpu.SemaphoreType.DMA((BLKS, 4)),
            ],
            compiler_params=pltpu.CompilerParams(
                collective_id=0, has_side_effects=True, vmem_limit_bytes=60 * 1024 * 1024),
        )(ao_blk, c_occ, c_virt)

    return jax.shard_map(
        local_block, mesh=mesh,
        in_specs=(P(("frag", "dev"), "dev2", None, None), P("frag", None), P("frag", None)),
        out_specs=P("frag", None, ("dev2", "dev")),
        check_vma=False)
```

time: 243 us -> 66.7 us (0.27)
  blocking collectives: 143 us -> 0 us
  local copies, waits for them, and re-layouts: 79.4 us -> 5.06 us
  Pallas kernels: 0 us -> 61.3 us
  matrix products: 19.3 us -> 0 us
    all_to_all x2 -> x0, blocking collectives: 143 us -> none  [the longest x1 94.6 us: local_block(): q_whole = lax.all_to_all(half_blk, 'dev2', 2, 1, tiled=True)]
    pallas_call x0 -> x1, Pallas kernels: none -> 61.3 us  [local_block(): pl.pallas_call(kernel, out_shape=jax.ShapeDtypeStruct((OCC, VIRT, LANES),...]
    all_to_all x4 -> x0, local copies, waits for them, and re-layouts: 33.4 us -> none  [the longest x3 31.8 us: local_block(): q_whole = lax.all_to_all(half_blk, 'dev2', 2, 1, tiled=True)]
    unnamed x6 -> x3, local copies, waits for them, and re-layouts: 30.3 us -> 5.06 us
    dot_general x3 -> x0, matrix products: 19.3 us -> none  [the longest x1 16.2 us: local_block(): jnp.einsum('pqsj,sb->pqjb', t_one, c_virt, preferred_element_type=jnp.flo...]
    reshape x1 -> x0, local copies, waits for them, and re-layouts: 15.7 us -> none  [local_block(): half_blk.reshape(ao_blk.shape[0], ao_blk.shape[1], occ_num * virt_num)]
where the time goes in v1:
time: 66.7 us; the launch traced here: 66.4 us
  Pallas kernels  61.3 us (92%)
  local copies, waits for them, and re-layouts  5.06 us (8%)
    pallas_call x1, Pallas kernels, local_block(): pl.pallas_call(kernel, out_shape=jax.ShapeDtypeStruct((OCC, VIRT, LANES),...  61.3 us
    unnamed x3, local copies, waits for them, and re-layouts  5.06 us

profile of v1, /device:TPU:0, one launch (start us, length us, event | category | flops | bytes accessed | tf_op | source)
XLA Modules:
  0.0 66.4 jit_solution(9227509668507206188)
XLA Ops:
  0.0 1.4 %copy.4.occ_ref = bf16[128,24]{1,0:T(8,128)(2,1)} copy(bf16[128,24]{0,1:T(8,128)(2,1)} %param.4) | data formatting | bytes 12288 | tf_op args[1]
  1.4 1.4 %copy.5.virt_ref = bf16[128,80]{1,0:T(8,128)(2,1)} copy(bf16[128,80]{0,1:T(8,128)(2,1)} %param.5) | data formatting | bytes 40960 | tf_op args[2]
  2.9 61.3 %shard_map.37 = f32[24,80,120]{2,1,0:T(8,128)} custom-call(bf16[32,32,128,128]{3,2,1,0:T(8,128)(2,1)} %ao_ref.1, bf16[128,24]{1,0:T(8,128)(2,1)} %copy.4.occ_ref, bf16[128,80]{1,0:T(8,128)(2,1)} %copy.5.virt_ref), custom_call_target="tpu_custom_call" | custom-call | tf_op jit(solution)/shard_map/pallas_call | solution.py:222
  64.2 2.2 %copy.7 = f32[24,80,120]{2,1,0:T(8,128)} copy(f32[24,80,120]{2,1,0:T(8,128)} %shard_map.37) | data formatting | bytes 1843200

commit v2 on v1

v2 whole, which is shorter than its diff:
```python
import functools

import jax
import jax.numpy as jnp
from jax import lax
from jax.experimental import pallas as pl
from jax.experimental.pallas import tpu as pltpu
from jax.sharding import PartitionSpec as P

MESH = pl.DeviceIdType.MESH
F32 = jnp.float32
BF16 = jnp.bfloat16
OCC = 24
VIRT = 80
LANES = 120
QSUB = 2
QBLK = 4
STEPS = 32 // QSUB
BLKS = 32 // QBLK
SUBS = QBLK // QSUB
SLOTS = 8
AHEAD = 6
LAG = 3


def dot(a, b):
    return jnp.dot(a, b, preferred_element_type=F32)


def dot_nt(a, b):
    return lax.dot_general(a, b, (((1,), (1,)), ((), ())), preferred_element_type=F32)


def iota(shape, dim):
    return lax.broadcasted_iota(jnp.int32, shape, dim)


def select(mask):
    return jnp.where(mask, 1.0, 0.0).astype(BF16)


def kernel(ao_ref, occ_ref, virt_ref, out_ref,
           a_buf, occ_lhs, virt_rhs, kron_own, kron_sib,
           h_buf, h_in, e_buf, y_in, e_all,
           a_sem, hs_sem, hr_sem, ys_sem, yr_sem, zs_sem, zr_sem):
    z = lax.axis_index("dev2")
    dev = lax.axis_index("dev")
    y = dev // 2
    core = dev % 2
    sib = y * 2 + (1 - core)
    across = (1 - y) * 2 + core
    half = z // 2
    order = (3 * (1 - half), 2 - half, 1 - z + 4 * half)

    def e_rows(blk, zz):
        return pl.ds(pl.multiple_of((zz * 32 + blk * QBLK) * OCC, 8), OCC * QBLK)

    def a_copy(s):
        return pltpu.make_async_copy(
            ao_ref.at[:, pl.ds(s * QSUB, QSUB)], a_buf.at[s % SLOTS], a_sem.at[s])

    def h_copy(s):
        return pltpu.make_async_remote_copy(
            src_ref=h_buf.at[1 - core, pl.ds(s * QSUB, QSUB)],
            dst_ref=h_in.at[pl.ds(s * QSUB, QSUB)],
            send_sem=hs_sem.at[s], recv_sem=hr_sem.at[s],
            device_id={"dev": sib}, device_id_type=MESH)

    def y_copy(blk, zz):
        return pltpu.make_async_remote_copy(
            src_ref=e_buf.at[1 - y, e_rows(blk, zz)], dst_ref=y_in.at[e_rows(blk, zz)],
            send_sem=ys_sem.at[blk, zz], recv_sem=yr_sem.at[blk, zz],
            device_id={"dev": across}, device_id_type=MESH)

    def z_copy(blk, zz, src):
        return pltpu.make_async_remote_copy(
            src_ref=e_buf.at[y, e_rows(blk, zz)], dst_ref=e_all.at[e_rows(blk, src)],
            send_sem=zs_sem.at[blk, zz], recv_sem=zr_sem.at[blk, src],
            device_id={"dev2": zz}, device_id_type=MESH)

    barrier = pltpu.get_barrier_semaphore()
    for peer in ({"dev": sib}, {"dev": across}, {"dev2": (z + 1) % 4}, {"dev2": (z + 2) % 4}, {"dev2": (z + 3) % 4}):
        pl.semaphore_signal(barrier, inc=1, device_id=peer, device_id_type=MESH)

    for s in range(AHEAD):
        a_copy(s).start()

    row = iota((OCC, OCC), 0)
    perm = select(iota((OCC, OCC), 1) == 3 * (row % 8) + row // 8)
    occ_t = dot(perm, occ_ref[...]).astype(BF16)
    zero = jnp.zeros((OCC, 128), BF16)
    occ_lhs[...] = jnp.concatenate(
        [jnp.concatenate([occ_t, zero], 1), jnp.concatenate([zero, occ_t], 1)], 0)
    row = iota((256, VIRT), 0)
    lane = row % 128
    pair = (row // 128) * LANES + lane
    for jj in range(3):
        pick = select((pair == jj * VIRT + iota((256, VIRT), 1)) & (lane < LANES))
        virt_rhs[:, pl.ds(jj * 128, 128)] = dot(pick, virt_ref[...]).astype(BF16)
    row = iota((192, OCC), 0)
    pick_i = select(row % OCC == iota((192, OCC), 1))
    occ_i = dot(pick_i, occ_ref[...]).astype(BF16)
    row = iota((192, 256), 0)
    keep = iota((192, 256), 1) % 8 == 2 * ((row % 96) // OCC) + row // 96
    for dst, who in ((kron_own, dev), (kron_sib, sib)):
        pick_p = select(iota((128, 256), 1) // 8 + who * 32 == iota((128, 256), 0))
        dst[...] = jnp.where(keep, dot(occ_i, pick_p), 0.0).astype(BF16)

    def half_step(s):
        for qq in range(QSUB):
            rows = []
            for p in range(0, 32, 4):
                a = [a_buf[s % SLOTS, p + k, qq] for k in range(4)]
                w = jnp.concatenate(
                    [jnp.concatenate(a[:2], 1), jnp.concatenate(a[2:], 1)], 0)
                r = dot(occ_lhs[...], w)
                for k in range(4):
                    part = r[(k // 2) * OCC:(k // 2 + 1) * OCC, (k % 2) * 128:(k % 2 + 1) * 128]
                    rows.append(jnp.concatenate([part[0:8], part[8:16], part[16:24]], 1))
            t_one = jnp.concatenate(rows, 0).astype(BF16)
            h = dot_nt(t_one, virt_rhs[...]).astype(BF16)
            h_buf[0, s * QSUB + qq] = h[:, :128]
            h_buf[1, s * QSUB + qq] = h[:, 128:]

    def e_step(s):
        q = s * QSUB
        own = jnp.concatenate([h_buf[core, q + k] for k in range(QSUB)], 1)
        other = jnp.concatenate([h_in[q + k] for k in range(QSUB)], 1)
        e = dot(kron_own[...], own) + dot(kron_sib[...], other)
        for k in range(QSUB):
            for yy in range(2):
                for zz in range(4):
                    r = (yy * 4 + zz) * OCC
                    e_buf[yy, pl.ds(pl.multiple_of((zz * 32 + q + k) * OCC, 8), OCC), :] = (
                        e[r:r + OCC, k * 128:(k + 1) * 128])

    def sum_block(blk):
        for zz in order:
            y_copy(blk, zz).wait_recv()
            rows = e_rows(blk, zz)
            e_buf[y, rows] = e_buf[y, rows] + y_in[rows]
            z_copy(blk, zz, z).start()
        y_copy(blk, z).wait_recv()
        rows = e_rows(blk, z)
        e_all[rows] = e_buf[y, rows] + y_in[rows]

    def step(s, carry):
        @pl.when(s < STEPS)
        def _():
            a_copy(s).wait()

            @pl.when(s + AHEAD < STEPS)
            def _():
                a_copy(s + AHEAD).start()
            half_step(s)

            @pl.when(s == 0)
            def _():
                pl.semaphore_wait(barrier, 5)
            h_copy(s).start()

        @pl.when((s > 0) & (s <= STEPS))
        def _():
            h_copy(s - 1).wait_recv()
            e_step(s - 1)

            @pl.when(s % SUBS == 0)
            def _():
                for zz in (*order, z):
                    y_copy(s // SUBS - 1, zz).start()

        @pl.when((s % SUBS == SUBS - 1) & (s // SUBS >= LAG))
        def _():
            sum_block(s // SUBS - LAG)
        return carry

    lax.fori_loop(0, STEPS + LAG * SUBS, step, 0)

    def arrived(blk, carry):
        for d in range(1, 4):
            z_copy(blk, z, (z + d) % 4).wait_recv()
        return carry

    lax.fori_loop(0, BLKS, arrived, 0)

    def v_step(n, carry):
        for pr in range(2):
            parts = []
            for k in range(2):
                i = n * 4 + pr * 2 + k
                e = e_all[pl.ds(i, 128, stride=OCC), :]
                hi = e.astype(BF16)
                rest = e - hi.astype(F32)
                mid = rest.astype(BF16)
                low = (rest - mid.astype(F32)).astype(BF16)
                parts.append((hi, mid, low))
            v = jnp.zeros((VIRT, 256), F32)
            for a, b in zip(*parts):
                v = v + dot(virt_ref[...], jnp.concatenate([a, b], 1))
            for k in range(2):
                out_ref[n * 4 + pr * 2 + k] = v[:, k * 128:k * 128 + LANES]
        return carry

    lax.fori_loop(0, OCC // 4, v_step, 0)

    def sent(s, carry):
        h_copy(s).wait_send()
        return carry

    lax.fori_loop(0, STEPS, sent, 0)

    def sent_blk(blk, carry):
        for zz in (*order, z):
            y_copy(blk, zz).wait_send()
        for zz in order:
            z_copy(blk, zz, z).wait_send()
        return carry

    lax.fori_loop(0, BLKS, sent_blk, 0)


def solution(mesh):
    def local_block(ao_blk, c_occ, c_virt):
        vmem = pl.BlockSpec(memory_space=pltpu.VMEM)
        return pl.pallas_call(
            kernel,
            out_shape=jax.ShapeDtypeStruct((OCC, VIRT, LANES), F32),
            in_specs=[pl.BlockSpec(memory_space=pl.ANY), vmem, vmem],
            out_specs=vmem,
            scratch_shapes=[
                pltpu.VMEM((SLOTS, 32, QSUB, 128, 128), BF16),
                pltpu.VMEM((2 * OCC, 256), BF16),
                pltpu.VMEM((256, 384), BF16),
                pltpu.VMEM((192, 256), BF16),
                pltpu.VMEM((192, 256), BF16),
                pltpu.VMEM((2, 32, 256, 128), BF16),
                pltpu.VMEM((32, 256, 128), BF16),
                pltpu.VMEM((2, 4 * 32 * OCC, 128), F32),
                pltpu.VMEM((4 * 32 * OCC, 128), F32),
                pltpu.VMEM((128 * OCC, 128), F32),
                pltpu.SemaphoreType.DMA((STEPS,)),
                pltpu.SemaphoreType.DMA((STEPS,)),
                pltpu.SemaphoreType.DMA((STEPS,)),
                pltpu.SemaphoreType.DMA((BLKS, 4)),
                pltpu.SemaphoreType.DMA((BLKS, 4)),
                pltpu.SemaphoreType.DMA((BLKS, 4)),
                pltpu.SemaphoreType.DMA((BLKS, 4)),
            ],
            compiler_params=pltpu.CompilerParams(
                collective_id=0, has_side_effects=True, vmem_limit_bytes=36 * 1024 * 1024),
        )(ao_blk, c_occ.T, c_virt.T)

    return jax.shard_map(
        local_block, mesh=mesh,
        in_specs=(P(("frag", "dev"), "dev2", None, None), P("frag", None), P("frag", None)),
        out_specs=P("frag", None, ("dev2", "dev")),
        check_vma=False)
```

time: 66.7 us -> 52.9 us (0.79)
  Pallas kernels: 61.3 us -> 50.3 us
  local copies, waits for them, and re-layouts: 5.06 us -> 2.36 us
    pallas_call x1, Pallas kernels: 61.3 us -> 50.3 us  [local_block(): pl.pallas_call(kernel, out_shape=jax.ShapeDtypeStruct((OCC, VIRT, LANES),...]
    unnamed x3 -> x5, local copies, waits for them, and re-layouts: 5.06 us -> 2.36 us
where the time goes in v2:
time: 52.9 us; the launch traced here: 52.7 us
  Pallas kernels  50.3 us (95%)
  local copies, waits for them, and re-layouts  2.36 us (4%)
    pallas_call x1, Pallas kernels, local_block(): pl.pallas_call(kernel, out_shape=jax.ShapeDtypeStruct((OCC, VIRT, LANES),...  50.3 us
    unnamed x5, local copies, waits for them, and re-layouts  2.36 us

profile of v2, /device:TPU:0, one launch (start us, length us, event | category | flops | bytes accessed | tf_op | source)
XLA Modules:
  0.0 52.7 jit_solution(441301223727665996)
XLA Ops:
  0.0 0.0 copy-start
  0.0 0.7 %copy-done = bf16[128,80]{0,1:T(8,128)(2,1)S(1)} copy-done((bf16[128,80]{0,1:T(8,128)(2,1)S(1)}, bf16[128,80]{0,1:T(8,128)(2,1)}, u32[]{:S(2)}) %copy-start) | copy-done | bytes 20504
  0.7 0.0 copy-start.1
  0.7 0.7 %copy-done.1 = bf16[128,24]{0,1:T(8,128)(2,1)S(1)} copy-done((bf16[128,24]{0,1:T(8,128)(2,1)S(1)}, bf16[128,24]{0,1:T(8,128)(2,1)}, u32[]{:S(2)}) %copy-start.1) | copy-done | bytes 6168
  1.4 50.3 %shard_map.37 = f32[24,80,120]{2,1,0:T(8,128)S(1)} custom-call(bf16[32,32,128,128]{3,2,1,0:T(8,128)(2,1)} %ao_ref.1, bf16[24,128]{1,0:T(8,128)(2,1)S(1)} %bitcast.3, bf16[80,128]{1,0:T(8,128)(2,1)S(1)} %bitcast.2), custom_call_target="tpu_custom_call" | custom-call | tf_op jit(solution)/shard_map/pallas_call | solution.py:225
  51.7 0.9 %copy.5 = f32[24,80,120]{2,1,0:T(8,128)} copy(f32[24,80,120]{2,1,0:T(8,128)S(1)} %shard_map.37) | data formatting | bytes 1843200
Async XLA Ops:
  0.0 0.7 %copy-start = (bf16[128,80]{0,1:T(8,128)(2,1)S(1)}, bf16[128,80]{0,1:T(8,128)(2,1)}, u32[]{:S(2)}) copy-start(bf16[128,80]{0,1:T(8,128)(2,1)} %param.5) | copy-start | bytes 61444
  0.7 0.7 %copy-start.1 = (bf16[128,24]{0,1:T(8,128)(2,1)S(1)}, bf16[128,24]{0,1:T(8,128)(2,1)}, u32[]{:S(2)}) copy-start(bf16[128,24]{0,1:T(8,128)(2,1)} %param.4) | copy-start | bytes 18436

commit v3 on v2

--- a/solution.py
+++ b/solution.py
@@ -20,7 +20,7 @@
 SUBS = QBLK // QSUB
 SLOTS = 8
 AHEAD = 6
-LAG = 3
+LAG = 2
 
 
 def dot(a, b):
@@ -39,10 +39,10 @@
     return jnp.where(mask, 1.0, 0.0).astype(BF16)
 
 
-def kernel(ao_ref, occ_ref, virt_ref, out_ref,
+def kernel(ao_ref, occ_hbm, virt_hbm, out_ref,
            a_buf, occ_lhs, virt_rhs, kron_own, kron_sib,
            h_buf, h_in, e_buf, y_in, e_all,
-           a_sem, hs_sem, hr_sem, ys_sem, yr_sem, zs_sem, zr_sem):
+           a_sem, hs_sem, hr_sem, ys_sem, yr_sem, zs_sem, zr_sem, c_sem, occ_ref, virt_ref):
     z = lax.axis_index("dev2")
     dev = lax.axis_index("dev")
     y = dev // 2
@@ -57,33 +57,38 @@
 
     def a_copy(s):
         return pltpu.make_async_copy(
-            ao_ref.at[:, pl.ds(s * QSUB, QSUB)], a_buf.at[s % SLOTS], a_sem.at[s])
+            ao_ref.at[:, pl.ds(s * QSUB, QSUB)], a_buf.at[s % SLOTS], a_sem.at[s % SLOTS])
 
     def h_copy(s):
         return pltpu.make_async_remote_copy(
             src_ref=h_buf.at[1 - core, pl.ds(s * QSUB, QSUB)],
             dst_ref=h_in.at[pl.ds(s * QSUB, QSUB)],
-            send_sem=hs_sem.at[s], recv_sem=hr_sem.at[s],
+            send_sem=hs_sem, recv_sem=hr_sem.at[s],
             device_id={"dev": sib}, device_id_type=MESH)
 
     def y_copy(blk, zz):
         return pltpu.make_async_remote_copy(
             src_ref=e_buf.at[1 - y, e_rows(blk, zz)], dst_ref=y_in.at[e_rows(blk, zz)],
-            send_sem=ys_sem.at[blk, zz], recv_sem=yr_sem.at[blk, zz],
+            send_sem=ys_sem, recv_sem=yr_sem.at[blk, zz],
             device_id={"dev": across}, device_id_type=MESH)
 
     def z_copy(blk, zz, src):
         return pltpu.make_async_remote_copy(
             src_ref=e_buf.at[y, e_rows(blk, zz)], dst_ref=e_all.at[e_rows(blk, src)],
-            send_sem=zs_sem.at[blk, zz], recv_sem=zr_sem.at[blk, src],
+            send_sem=zs_sem, recv_sem=zr_sem,
             device_id={"dev2": zz}, device_id_type=MESH)
 
     barrier = pltpu.get_barrier_semaphore()
     for peer in ({"dev": sib}, {"dev": across}, {"dev2": (z + 1) % 4}, {"dev2": (z + 2) % 4}, {"dev2": (z + 3) % 4}):
         pl.semaphore_signal(barrier, inc=1, device_id=peer, device_id_type=MESH)
 
+    c_copies = (pltpu.make_async_copy(occ_hbm, occ_ref, c_sem.at[0]), pltpu.make_async_copy(virt_hbm, virt_ref, c_sem.at[1]))
+    for c in c_copies:
+        c.start()
     for s in range(AHEAD):
         a_copy(s).start()
+    for c in c_copies:
+        c.wait()
 
     row = iota((OCC, OCC), 0)
     perm = select(iota((OCC, OCC), 1) == 3 * (row % 8) + row // 8)
@@ -176,12 +181,11 @@
 
     lax.fori_loop(0, STEPS + LAG * SUBS, step, 0)
 
-    def arrived(blk, carry):
-        for d in range(1, 4):
-            z_copy(blk, z, (z + d) % 4).wait_recv()
-        return carry
-
-    lax.fori_loop(0, BLKS, arrived, 0)
+    part = pl.ds(0, 3 * 32 * OCC)
+    arrivals = pltpu.make_async_remote_copy(
+        src_ref=e_buf.at[y, part], dst_ref=e_all.at[part], send_sem=zs_sem, recv_sem=zr_sem,
+        device_id={"dev2": (z + 1) % 4}, device_id_type=MESH)
+    arrivals.wait_recv()
 
     def v_step(n, carry):
         for pr in range(2):
@@ -203,20 +207,13 @@
 
     lax.fori_loop(0, OCC // 4, v_step, 0)
 
-    def sent(s, carry):
-        h_copy(s).wait_send()
-        return carry
-
-    lax.fori_loop(0, STEPS, sent, 0)
-
-    def sent_blk(blk, carry):
-        for zz in (*order, z):
-            y_copy(blk, zz).wait_send()
-        for zz in order:
-            z_copy(blk, zz, z).wait_send()
-        return carry
-
-    lax.fori_loop(0, BLKS, sent_blk, 0)
+    pltpu.make_async_remote_copy(
+        src_ref=h_buf.at[1 - core], dst_ref=h_in, send_sem=hs_sem, recv_sem=hr_sem.at[0],
+        device_id={"dev": sib}, device_id_type=MESH).wait_send()
+    pltpu.make_async_remote_copy(
+        src_ref=e_buf.at[1 - y], dst_ref=y_in, send_sem=ys_sem, recv_sem=yr_sem.at[0, 0],
+        device_id={"dev": across}, device_id_type=MESH).wait_send()
+    arrivals.wait_send()
 
 
 def solution(mesh):
@@ -225,7 +222,7 @@
         return pl.pallas_call(
             kernel,
             out_shape=jax.ShapeDtypeStruct((OCC, VIRT, LANES), F32),
-            in_specs=[pl.BlockSpec(memory_space=pl.ANY), vmem, vmem],
+            in_specs=[pl.BlockSpec(memory_space=pltpu.HBM)] * 3,
             out_specs=vmem,
             scratch_shapes=[
                 pltpu.VMEM((SLOTS, 32, QSUB, 128, 128), BF16),
@@ -238,13 +235,16 @@
                 pltpu.VMEM((2, 4 * 32 * OCC, 128), F32),
                 pltpu.VMEM((4 * 32 * OCC, 128), F32),
                 pltpu.VMEM((128 * OCC, 128), F32),
+                pltpu.SemaphoreType.DMA((SLOTS,)),
+                pltpu.SemaphoreType.DMA,
                 pltpu.SemaphoreType.DMA((STEPS,)),
-                pltpu.SemaphoreType.DMA((STEPS,)),
-                pltpu.SemaphoreType.DMA((STEPS,)),
+                pltpu.SemaphoreType.DMA,
                 pltpu.SemaphoreType.DMA((BLKS, 4)),
-                pltpu.SemaphoreType.DMA((BLKS, 4)),
-                pltpu.SemaphoreType.DMA((BLKS, 4)),
-                pltpu.SemaphoreType.DMA((BLKS, 4)),
+                pltpu.SemaphoreType.DMA,
+                pltpu.SemaphoreType.DMA,
+                pltpu.SemaphoreType.DMA((2,)),
+                pltpu.VMEM((OCC, 128), BF16),
+                pltpu.VMEM((VIRT, 128), BF16),
             ],
             compiler_params=pltpu.CompilerParams(
                 collective_id=0, has_side_effects=True, vmem_limit_bytes=36 * 1024 * 1024),

time: 52.9 us -> 51.8 us (0.979)
  Pallas kernels: 50.3 us -> 49.2 us
    pallas_call x1, Pallas kernels: 50.3 us -> 49.2 us  [local_block(): pl.pallas_call(kernel, out_shape=jax.ShapeDtypeStruct((OCC, VIRT, LANES),...]
where the time goes in v3:
time: 51.8 us; the launch traced here: 51.6 us
  Pallas kernels  49.2 us (95%)
  local copies, waits for them, and re-layouts  2.36 us (5%)
    pallas_call x1, Pallas kernels, local_block(): pl.pallas_call(kernel, out_shape=jax.ShapeDtypeStruct((OCC, VIRT, LANES),...  49.2 us
    unnamed x5, local copies, waits for them, and re-layouts  2.36 us

profile of v3, /device:TPU:0, one launch (start us, length us, event | category | flops | bytes accessed | tf_op | source)
XLA Modules:
  0.0 51.6 jit_solution(15363337763831824553)
XLA Ops:
  0.0 0.0 copy-start
  0.0 0.7 %copy-done = bf16[128,80]{0,1:T(8,128)(2,1)S(1)} copy-done((bf16[128,80]{0,1:T(8,128)(2,1)S(1)}, bf16[128,80]{0,1:T(8,128)(2,1)}, u32[]{:S(2)}) %copy-start) | copy-done | bytes 20504
  0.7 0.0 copy-start.1
  0.7 0.7 %copy-done.1 = bf16[128,24]{0,1:T(8,128)(2,1)S(1)} copy-done((bf16[128,24]{0,1:T(8,128)(2,1)S(1)}, bf16[128,24]{0,1:T(8,128)(2,1)}, u32[]{:S(2)}) %copy-start.1) | copy-done | bytes 6168
  1.4 49.2 %shard_map.37 = f32[24,80,120]{2,1,0:T(8,128)S(1)} custom-call(bf16[32,32,128,128]{3,2,1,0:T(8,128)(2,1)} %ao_ref.1, bf16[24,128]{1,0:T(8,128)(2,1)S(1)} %bitcast.3, bf16[80,128]{1,0:T(8,128)(2,1)S(1)} %bitcast.2), custom_call_target="tpu_custom_call" | custom-call | tf_op jit(solution)/shard_map/pallas_call | solution.py:222
  50.6 0.9 %copy.5 = f32[24,80,120]{2,1,0:T(8,128)} copy(f32[24,80,120]{2,1,0:T(8,128)S(1)} %shard_map.37) | data formatting | bytes 1843200
Async XLA Ops:
  0.0 0.7 %copy-start = (bf16[128,80]{0,1:T(8,128)(2,1)S(1)}, bf16[128,80]{0,1:T(8,128)(2,1)}, u32[]{:S(2)}) copy-start(bf16[128,80]{0,1:T(8,128)(2,1)} %param.5) | copy-start | bytes 61444
  0.7 0.7 %copy-start.1 = (bf16[128,24]{0,1:T(8,128)(2,1)S(1)}, bf16[128,24]{0,1:T(8,128)(2,1)}, u32[]{:S(2)}) copy-start(bf16[128,24]{0,1:T(8,128)(2,1)} %param.4) | copy-start | bytes 18436

commit v4 on v0

v4 whole, which is shorter than its diff:
```python
import functools

import jax
import jax.numpy as jnp
from jax import lax
from jax.experimental import pallas as pl
from jax.experimental.pallas import tpu as pltpu
from jax.sharding import PartitionSpec as P

MESH = pl.DeviceIdType.MESH
F32 = jnp.float32
BF16 = jnp.bfloat16
OCC = 24
VIRT = 80
LANES = 120
SPECIAL = 2
KEPT = 32 - SPECIAL
RIDERS = KEPT // SPECIAL
FREE = 128 - LANES
PART = 32 * OCC
STEPS = 17
LATE = 7
SLOTS = 16
AHEAD = 6
QGRP = 8
GROUPS = 4
H_RING = 4
Y_RING = 8
CHUNKS = ((0, 8), (8, 8), (16, 8), (24, 6))
CROSS_SUM = 4
NEAR_AT = (10, 13, 16, 18)
NEAR_SUM = (14, 17, 20, 22)
OWN_AT = (14, 17, 19, 20)
V_AT = (18, 21, 24)
END = 25


def dot(a, b):
    return jnp.dot(a, b, preferred_element_type=F32)


def dot_nt(a, b):
    return lax.dot_general(a, b, (((1,), (1,)), ((), ())), preferred_element_type=F32)


def iota(shape, dim):
    return lax.broadcasted_iota(jnp.int32, shape, dim)


def select(mask):
    return jnp.where(mask, 1.0, 0.0).astype(BF16)


def kernel(ao_ref, occ_hbm, virt_hbm, out_ref,
           a_buf, a_late, occ_lhs, virt_rhs, kron_own, kron_sib, virt_v,
           h_buf, h_in, e_special, e_buf, y_in, e_all, occ_ref, virt_ref,
           c_sem, a_sem, al_sem, hs_sem, hr_sem, hl_sem, ys_sem, yc_sem, yn_sem, yo_sem,
           zs_sem, zc_sem, zn_sem):
    z = lax.axis_index("dev2")
    dev = lax.axis_index("dev")
    y = dev // 2
    core = dev % 2
    sib = y * 2 + (1 - core)
    across = (1 - y) * 2 + core
    half = z // 2
    far = 3 * (1 - half)
    far_near = 2 - half
    near = 1 - z + 4 * half

    def rows_of(q, n):
        if not isinstance(q, int):
            q = pl.multiple_of(q * OCC, 8)
        else:
            q = q * OCC
        return pl.ds(q, n * OCC)

    def a_copy(q, n, s):
        return pltpu.make_async_copy(
            ao_ref.at[:, pl.ds(q, n)], a_buf.at[:, pl.ds(q % SLOTS, n)], a_sem.at[s % 8])

    a_copy_late = pltpu.make_async_copy(ao_ref.at[:, 31], a_late, al_sem)

    def h_copy(q, n, sem):
        return pltpu.make_async_remote_copy(
            src_ref=h_buf.at[1 - core, pl.ds(q, n)], dst_ref=h_in.at[pl.ds(q, n)],
            send_sem=hs_sem, recv_sem=sem,
            device_id={"dev": sib}, device_id_type=MESH)

    def y_copy(z0, zn, q, n, sem):
        return pltpu.make_async_remote_copy(
            src_ref=e_buf.at[1 - y, pl.ds(z0, zn), rows_of(q, n)],
            dst_ref=y_in.at[pl.ds(z0, zn), rows_of(q, n)],
            send_sem=ys_sem, recv_sem=sem,
            device_id={"dev": across}, device_id_type=MESH)

    def y_cross(q, n, s):
        return y_copy(2 * (1 - half), 2, q, n, yc_sem.at[s % Y_RING])

    def y_near(k):
        return y_copy(near, 1, *CHUNKS[k], yn_sem.at[k])

    def y_own(k):
        return y_copy(z, 1, *CHUNKS[k], yo_sem.at[k])

    def add_send(zz, q, n, sem):
        rows = rows_of(q, n)
        e_buf[y, zz, rows] = e_buf[y, zz, rows] + y_in[zz, rows]
        pltpu.make_async_remote_copy(
            src_ref=e_buf.at[y, zz, rows], dst_ref=e_all.at[rows_of(z * 32 + q, n)],
            send_sem=zs_sem, recv_sem=sem,
            device_id={"dev2": zz}, device_id_type=MESH).start()

    def z_wait(n, sem):
        rows = pl.ds(0, n * OCC)
        pltpu.make_async_remote_copy(
            src_ref=e_all.at[rows], dst_ref=e_all.at[rows], send_sem=zs_sem, recv_sem=sem,
            device_id={"dev2": near}, device_id_type=MESH).wait_recv()

    def when_step(s, first, end, shift, do):
        t = s - shift

        if first == 0:
            @pl.when(t == 0)
            def _():
                do(30, 1, 0)

        @pl.when((t == 1) | (t == 2))
        def _():
            do(t - 1, 1, t)

        @pl.when((t > 2) & (t < end))
        def _():
            do(2 * t - 4, 2, t)

    barrier = pltpu.get_barrier_semaphore()
    for peer in ({"dev": sib}, {"dev": across}, {"dev2": (z + 1) % 4}, {"dev2": (z + 2) % 4}, {"dev2": (z + 3) % 4}):
        pl.semaphore_signal(barrier, inc=1, device_id=peer, device_id_type=MESH)

    c_copies = (pltpu.make_async_copy(occ_hbm, occ_ref, c_sem.at[0]),
                pltpu.make_async_copy(virt_hbm, virt_ref, c_sem.at[1]))
    for c in c_copies:
        c.start()
    a_copy(30, 1, 0).start()
    for i in range(OCC):
        out_ref[i] = jnp.zeros((VIRT, LANES), F32)
    for c in c_copies:
        c.wait()
    for s in range(1, AHEAD):
        a_copy(*((s - 1, 1) if s < 3 else (2 * s - 4, 2)), s).start()

    row = iota((OCC, OCC), 0)
    perm = select(iota((OCC, OCC), 1) == 3 * (row % 8) + row // 8)
    occ_t = dot(perm, occ_ref[...]).astype(BF16)
    zero = jnp.zeros((OCC, 128), BF16)
    occ_lhs[...] = jnp.concatenate(
        [jnp.concatenate([occ_t, zero], 1), jnp.concatenate([zero, occ_t], 1)], 0)
    row = iota((256, VIRT), 0)
    lane = row % 128
    pair = (row // 128) * LANES + lane
    for jj in range(3):
        pick = select((pair == jj * VIRT + iota((256, VIRT), 1)) & (lane < LANES))
        virt_rhs[:, pl.ds(jj * 128, 128)] = dot(pick, virt_ref[...]).astype(BF16)
    row = iota((192, OCC), 0)
    pick_i = select(row % OCC == iota((192, OCC), 1))
    occ_i = dot(pick_i, occ_ref[...]).astype(BF16)
    row = iota((192, 256), 0)
    keep = iota((192, 256), 1) % 8 == 2 * ((row % 96) // OCC) + row // 96
    for dst, who in ((kron_own, dev), (kron_sib, sib)):
        pick_p = select(iota((128, 256), 1) // 8 + who * 32 == iota((128, 256), 0))
        dst[...] = jnp.where(keep, dot(occ_i, pick_p), 0.0).astype(BF16)
    col = iota((128, 96), 1)
    for g in range(GROUPS):
        pick_q = select(iota((128, 96), 0) == (col % 32) // QGRP * 32 + g * QGRP + col % QGRP)
        virt_v[g] = dot(virt_ref[...], pick_q).astype(BF16)

    def half_step(tiles, q, n):
        for qq in range(n):
            rows = []
            for p in range(0, 32, 4):
                a = [tiles(p + k, qq) for k in range(4)]
                w = jnp.concatenate(
                    [jnp.concatenate(a[:2], 1), jnp.concatenate(a[2:], 1)], 0)
                r = dot(occ_lhs[...], w)
                for k in range(4):
                    part = r[(k // 2) * OCC:(k // 2 + 1) * OCC, (k % 2) * 128:(k % 2 + 1) * 128]
                    rows.append(jnp.concatenate([part[0:8], part[8:16], part[16:24]], 1))
            t_one = jnp.concatenate(rows, 0).astype(BF16)
            h = dot_nt(t_one, virt_rhs[...]).astype(BF16)
            h_buf[0, q + qq] = h[:, :128]
            h_buf[1, q + qq] = h[:, 128:]

    def contract_p(q, n):
        own = jnp.concatenate([h_buf[core, q + k] for k in range(n)], 1)
        other = jnp.concatenate([h_in[q + k] for k in range(n)], 1)
        return dot(kron_own[...], own) + dot(kron_sib[...], other)

    def e_step(q, n):
        e = contract_p(q, n)
        free = iota((192, 128), 1) >= LANES
        for k in range(n):
            at = (q + k) % RIDERS * FREE
            rider = pltpu.roll(e_special[(q + k) // RIDERS], LANES - at, 1)
            row = jnp.where(free, rider, e[:, k * 128:(k + 1) * 128])
            for yy in range(2):
                for zz in range(4):
                    r = (yy * 4 + zz) * OCC
                    e_buf[yy, zz, rows_of(q + k, 1), :] = row[r:r + OCC]

    def unpack(sp, first, end):
        lane = iota((8, 128), 1)
        for src in range(4):
            for ib in range(0, OCC, 8):
                dst = pl.ds((src * 32 + KEPT + sp) * OCC + ib, 8)
                acc = e_all[dst] if first else jnp.zeros((8, 128), F32)
                for k in range(first, end):
                    row = e_all[pl.ds((src * 32 + sp * RIDERS + k) * OCC + ib, 8)]
                    acc = jnp.where(lane // FREE == k, pltpu.roll(row, (k + 1) * FREE % 128, 1), acc)
                e_all[dst] = acc

    def v_group(g):
        lhs = virt_v[g]
        for i in range(0, OCC, 2):
            parts = []
            for k in range(2):
                e = jnp.concatenate(
                    [e_all[pl.ds((src * 32 + g * QGRP) * OCC + i + k, QGRP, stride=OCC), :] for src in range(4)], 0)
                hi = e.astype(BF16)
                rest = e - hi.astype(F32)
                mid = rest.astype(BF16)
                low = (rest - mid.astype(F32)).astype(BF16)
                parts.append(jnp.concatenate([hi, mid, low], 0))
            v = dot(lhs, jnp.concatenate(parts, 1))
            for k in range(2):
                out_ref[i + k] += v[:, k * 128:k * 128 + LANES]

    def finish(g):
        y_own(g).wait_recv()
        q, n = CHUNKS[g]
        rows = rows_of(q, n)
        e_all[rows_of(z * 32 + q, n)] = e_buf[y, z, rows] + y_in[z, rows]
        z_wait(n, zn_sem.at[g])
        z_wait(2 * n, zc_sem.at[g])
        if g == 1:
            unpack(0, 0, 15)
        if g == 2:
            unpack(1, 0, 9)
        if g == 3:
            unpack(1, 9, 15)
        v_group(g)

    def step(s, carry):
        def transform(q, n, t):
            a_copy(q, n, t).wait()

            @pl.when(t + AHEAD < STEPS)
            def _():
                a_copy(2 * (t + AHEAD) - 4, 2, t + AHEAD).start()
            slot = q % SLOTS
            half_step(lambda p, qq: a_buf[p, slot + qq], q, n)
            if isinstance(q, int):
                pl.semaphore_wait(barrier, 5)
            h_copy(q, n, hr_sem.at[t % H_RING]).start()

        when_step(s, 0, STEPS, 0, transform)

        @pl.when(s == 2)
        def _():
            a_copy_late.start()

        @pl.when(s == LATE)
        def _():
            a_copy_late.wait()
            half_step(lambda p, qq: a_late[p], 31, 1)
            h_copy(31, 1, hl_sem).start()

        def to_e(q, n, t):
            h_copy(q, n, hr_sem.at[t % H_RING]).wait_recv()
            if isinstance(q, int):
                e_special[0] = contract_p(30, 1)
            else:
                e_step(q, n)
                y_cross(q, n, t).start()

        when_step(s, 0, STEPS, 1, to_e)

        @pl.when(s == LATE + 1)
        def _():
            h_copy(31, 1, hl_sem).wait_recv()
            e_special[1] = contract_p(31, 1)

        for k in range(GROUPS):
            @pl.when(s == NEAR_AT[k])
            def _():
                y_near(k).start()

            @pl.when(s == OWN_AT[k])
            def _():
                y_own(k).start()

        def to_z(q, n, t):
            y_cross(q, n, t).wait_recv()
            add_send(far, q, n, zc_sem.at[q // QGRP])
            add_send(far_near, q, n, zc_sem.at[q // QGRP])

        when_step(s, 1, STEPS, CROSS_SUM - 1, to_z)

        for k in range(GROUPS):
            @pl.when(s == NEAR_SUM[k])
            def _():
                y_near(k).wait_recv()
                add_send(near, *CHUNKS[k], zn_sem.at[k])

        for g in range(GROUPS - 1):
            @pl.when(s == V_AT[g])
            def _():
                finish(g)
        return carry

    lax.fori_loop(0, END, step, 0)
    finish(GROUPS - 1)

    pltpu.make_async_remote_copy(
        src_ref=h_buf.at[1 - core], dst_ref=h_in, send_sem=hs_sem, recv_sem=hl_sem,
        device_id={"dev": sib}, device_id_type=MESH).wait_send()
    y_copy(0, 4, 0, KEPT, yo_sem.at[0]).wait_send()
    rows = pl.ds(0, 3 * KEPT * OCC)
    pltpu.make_async_remote_copy(
        src_ref=e_all.at[rows], dst_ref=e_all.at[rows], send_sem=zs_sem, recv_sem=zn_sem.at[0],
        device_id={"dev2": near}, device_id_type=MESH).wait_send()


def solution(mesh):
    def local_block(ao_blk, c_occ, c_virt):
        hbm = pl.BlockSpec(memory_space=pltpu.HBM)
        dma = pltpu.SemaphoreType.DMA
        return pl.pallas_call(
            kernel,
            out_shape=jax.ShapeDtypeStruct((OCC, VIRT, LANES), F32),
            in_specs=[hbm, hbm, hbm],
            out_specs=pl.BlockSpec(memory_space=pltpu.VMEM),
            scratch_shapes=[
                pltpu.VMEM((32, SLOTS, 128, 128), BF16),
                pltpu.VMEM((32, 128, 128), BF16),
                pltpu.VMEM((2 * OCC, 256), BF16),
                pltpu.VMEM((256, 384), BF16),
                pltpu.VMEM((192, 256), BF16),
                pltpu.VMEM((192, 256), BF16),
                pltpu.VMEM((GROUPS, VIRT, 96), BF16),
                pltpu.VMEM((2, 32, 256, 128), BF16),
                pltpu.VMEM((32, 256, 128), BF16),
                pltpu.VMEM((SPECIAL, 192, 128), F32),
                pltpu.VMEM((2, 4, PART, 128), F32),
                pltpu.VMEM((4, PART, 128), F32),
                pltpu.VMEM((4 * PART, 128), F32),
                pltpu.VMEM((OCC, 128), BF16),
                pltpu.VMEM((VIRT, 128), BF16),
                dma((2,)), dma((8,)), dma,
                dma, dma((H_RING,)), dma,
                dma, dma((Y_RING,)), dma((GROUPS,)), dma((GROUPS,)),
                dma, dma((GROUPS,)), dma((GROUPS,)),
            ],
            compiler_params=pltpu.CompilerParams(
                collective_id=0, has_side_effects=True, vmem_limit_bytes=37 * 1024 * 1024),
        )(ao_blk, *(pltpu.with_memory_space_constraint(c.T, pltpu.HBM) for c in (c_occ, c_virt)))

    return jax.shard_map(
        local_block, mesh=mesh,
        in_specs=(P(("frag", "dev"), "dev2", None, None), P("frag", None), P("frag", None)),
        out_specs=P("frag", None, ("dev2", "dev")),
        check_vma=False)
```

time: 243 us -> 46.6 us (0.19)
  blocking collectives: 143 us -> 0 us
  local copies, waits for them, and re-layouts: 79.4 us -> 0.95 us
  Pallas kernels: 0 us -> 45.5 us
  matrix products: 19.3 us -> 0 us
    all_to_all x2 -> x0, blocking collectives: 143 us -> none  [the longest x1 94.6 us: local_block(): q_whole = lax.all_to_all(half_blk, 'dev2', 2, 1, tiled=True)]
    pallas_call x0 -> x1, Pallas kernels: none -> 45.5 us  [local_block(): pl.pallas_call(kernel, out_shape=jax.ShapeDtypeStruct((OCC, VIRT, LANES),...]
    all_to_all x4 -> x0, local copies, waits for them, and re-layouts: 33.4 us -> none  [the longest x3 31.8 us: local_block(): q_whole = lax.all_to_all(half_blk, 'dev2', 2, 1, tiled=True)]
    unnamed x6 -> x1, local copies, waits for them, and re-layouts: 30.3 us -> 0.95 us
    dot_general x3 -> x0, matrix products: 19.3 us -> none  [the longest x1 16.2 us: local_block(): jnp.einsum('pqsj,sb->pqjb', t_one, c_virt, preferred_element_type=jnp.flo...]
    reshape x1 -> x0, local copies, waits for them, and re-layouts: 15.7 us -> none  [local_block(): half_blk.reshape(ao_blk.shape[0], ao_blk.shape[1], occ_num * virt_num)]
where the time goes in v4:
time: 46.6 us; the launch traced here: 46.5 us
  Pallas kernels  45.5 us (98%)
  local copies, waits for them, and re-layouts  0.95 us (2%)
    pallas_call x1, Pallas kernels, local_block(): pl.pallas_call(kernel, out_shape=jax.ShapeDtypeStruct((OCC, VIRT, LANES),...  45.5 us
    unnamed x1, local copies, waits for them, and re-layouts  0.95 us

profile of v4, /device:TPU:0, one launch (start us, length us, event | category | flops | bytes accessed | tf_op | source)
XLA Modules:
  0.0 46.5 jit_solution(9480411957890521600)
XLA Ops:
  0.0 45.5 %shard_map.37 = f32[24,80,120]{2,1,0:T(8,128)S(1)} custom-call(bf16[32,32,128,128]{3,2,1,0:T(8,128)(2,1)} %ao_ref.1, bf16[24,128]{1,0:T(8,128)(2,1)} %bitcast.3, bf16[80,128]{1,0:T(8,128)(2,1)} %bitcast.2), custom_call_target="tpu_custom_call" | custom-call | tf_op jit(solution)/shard_map/pallas_call | solution.py:336
  45.5 0.9 %copy.5 = f32[24,80,120]{2,1,0:T(8,128)} copy(f32[24,80,120]{2,1,0:T(8,128)S(1)} %shard_map.37) | data formatting | bytes 1843200

commit v5 on v4

--- a/solution.py
+++ b/solution.py
@@ -19,20 +19,23 @@
 FREE = 128 - LANES
 PART = 32 * OCC
 STEPS = 17
-LATE = 7
+LATE = 9
 SLOTS = 16
 AHEAD = 6
 QGRP = 8
 GROUPS = 4
 H_RING = 4
 Y_RING = 8
-CHUNKS = ((0, 8), (8, 8), (16, 8), (24, 6))
-CROSS_SUM = 4
-NEAR_AT = (10, 13, 16, 18)
-NEAR_SUM = (14, 17, 20, 22)
-OWN_AT = (14, 17, 19, 20)
-V_AT = (18, 21, 24)
-END = 25
+OWN = ((0, 8), (8, 8), (16, 8), (24, 6))
+NEAR = ((0, 4), (4, 4), (8, 8), (16, 8), (24, 6))
+SWITCH = 4
+CROSS_SUM = 3
+CROSS_SUM_2 = 4
+NEAR_AT = (7, 8, 11, 15, 17)
+NEAR_SUM = (11, 12, 15, 19, 21)
+OWN_AT = (17, 17, 18, 19)
+V_AT = (21, 22, 23)
+END = 24
 
 
 def dot(a, b):
@@ -97,10 +100,10 @@
         return y_copy(2 * (1 - half), 2, q, n, yc_sem.at[s % Y_RING])
 
     def y_near(k):
-        return y_copy(near, 1, *CHUNKS[k], yn_sem.at[k])
+        return y_copy(near, 1, *NEAR[k], yn_sem.at[k])
 
     def y_own(k):
-        return y_copy(z, 1, *CHUNKS[k], yo_sem.at[k])
+        return y_copy(z, 1, *OWN[k], yo_sem.at[k])
 
     def add_send(zz, q, n, sem):
         rows = rows_of(q, n)
@@ -124,11 +127,12 @@
             def _():
                 do(30, 1, 0)
 
-        @pl.when((t == 1) | (t == 2))
-        def _():
-            do(t - 1, 1, t)
-
-        @pl.when((t > 2) & (t < end))
+        if first < 3:
+            @pl.when((t == 1) | (t == 2))
+            def _():
+                do(t - 1, 1, t)
+
+        @pl.when((t >= max(first, 3)) & (t < end))
         def _():
             do(2 * t - 4, 2, t)
 
@@ -159,7 +163,7 @@
     pair = (row // 128) * LANES + lane
     for jj in range(3):
         pick = select((pair == jj * VIRT + iota((256, VIRT), 1)) & (lane < LANES))
-        virt_rhs[:, pl.ds(jj * 128, 128)] = dot(pick, virt_ref[...]).astype(BF16)
+        virt_rhs[pl.ds(jj * 128, 128), :] = lax.dot_general(virt_ref[...], pick, (((0,), (1,)), ((), ())), preferred_element_type=F32).astype(BF16)
     row = iota((192, OCC), 0)
     pick_i = select(row % OCC == iota((192, OCC), 1))
     occ_i = dot(pick_i, occ_ref[...]).astype(BF16)
@@ -174,8 +178,8 @@
         virt_v[g] = dot(virt_ref[...], pick_q).astype(BF16)
 
     def half_step(tiles, q, n):
+        rows = []
         for qq in range(n):
-            rows = []
             for p in range(0, 32, 4):
                 a = [tiles(p + k, qq) for k in range(4)]
                 w = jnp.concatenate(
@@ -184,10 +188,11 @@
                 for k in range(4):
                     part = r[(k // 2) * OCC:(k // 2 + 1) * OCC, (k % 2) * 128:(k % 2 + 1) * 128]
                     rows.append(jnp.concatenate([part[0:8], part[8:16], part[16:24]], 1))
-            t_one = jnp.concatenate(rows, 0).astype(BF16)
-            h = dot_nt(t_one, virt_rhs[...]).astype(BF16)
-            h_buf[0, q + qq] = h[:, :128]
-            h_buf[1, q + qq] = h[:, 128:]
+        t_one = jnp.concatenate(rows, 0).astype(BF16)
+        h = dot(t_one, virt_rhs[...]).astype(BF16)
+        for qq in range(n):
+            h_buf[0, q + qq] = h[qq * 256:(qq + 1) * 256, :128]
+            h_buf[1, q + qq] = h[qq * 256:(qq + 1) * 256, 128:]
 
     def contract_p(q, n):
         own = jnp.concatenate([h_buf[core, q + k] for k in range(n)], 1)
@@ -235,7 +240,7 @@
 
     def finish(g):
         y_own(g).wait_recv()
-        q, n = CHUNKS[g]
+        q, n = OWN[g]
         rows = rows_of(q, n)
         e_all[rows_of(z * 32 + q, n)] = e_buf[y, z, rows] + y_in[z, rows]
         z_wait(n, zn_sem.at[g])
@@ -273,6 +278,11 @@
             half_step(lambda p, qq: a_late[p], 31, 1)
             h_copy(31, 1, hl_sem).start()
 
+        @pl.when(s == LATE + 1)
+        def _():
+            h_copy(31, 1, hl_sem).wait_recv()
+            e_special[1] = contract_p(31, 1)
+
         def to_e(q, n, t):
             h_copy(q, n, hr_sem.at[t % H_RING]).wait_recv()
             if isinstance(q, int):
@@ -283,16 +293,12 @@
 
         when_step(s, 0, STEPS, 1, to_e)
 
-        @pl.when(s == LATE + 1)
-        def _():
-            h_copy(31, 1, hl_sem).wait_recv()
-            e_special[1] = contract_p(31, 1)
+        for k in range(len(NEAR)):
+            @pl.when(s == NEAR_AT[k])
+            def _():
+                y_near(k).start()
 
         for k in range(GROUPS):
-            @pl.when(s == NEAR_AT[k])
-            def _():
-                y_near(k).start()
-
             @pl.when(s == OWN_AT[k])
             def _():
                 y_own(k).start()
@@ -302,13 +308,14 @@
             add_send(far, q, n, zc_sem.at[q // QGRP])
             add_send(far_near, q, n, zc_sem.at[q // QGRP])
 
-        when_step(s, 1, STEPS, CROSS_SUM - 1, to_z)
-
-        for k in range(GROUPS):
+        when_step(s, 1, SWITCH, CROSS_SUM, to_z)
+        when_step(s, SWITCH, STEPS, CROSS_SUM_2, to_z)
+
+        for k in range(len(NEAR)):
             @pl.when(s == NEAR_SUM[k])
             def _():
                 y_near(k).wait_recv()
-                add_send(near, *CHUNKS[k], zn_sem.at[k])
+                add_send(near, *NEAR[k], zn_sem.at[NEAR[k][0] // QGRP])
 
         for g in range(GROUPS - 1):
             @pl.when(s == V_AT[g])
@@ -342,7 +349,7 @@
                 pltpu.VMEM((32, SLOTS, 128, 128), BF16),
                 pltpu.VMEM((32, 128, 128), BF16),
                 pltpu.VMEM((2 * OCC, 256), BF16),
-                pltpu.VMEM((256, 384), BF16),
+                pltpu.VMEM((384, 256), BF16),
                 pltpu.VMEM((192, 256), BF16),
                 pltpu.VMEM((192, 256), BF16),
                 pltpu.VMEM((GROUPS, VIRT, 96), BF16),
@@ -356,7 +363,7 @@
                 pltpu.VMEM((VIRT, 128), BF16),
                 dma((2,)), dma((8,)), dma,
                 dma, dma((H_RING,)), dma,
-                dma, dma((Y_RING,)), dma((GROUPS,)), dma((GROUPS,)),
+                dma, dma((Y_RING,)), dma((len(NEAR),)), dma((GROUPS,)),
                 dma, dma((GROUPS,)), dma((GROUPS,)),
             ],
             compiler_params=pltpu.CompilerParams(

time: 46.6 us -> 45 us (0.966)
  Pallas kernels: 45.5 us -> 43.9 us
    pallas_call x1, Pallas kernels: 45.5 us -> 43.9 us  [local_block(): pl.pallas_call(kernel, out_shape=jax.ShapeDtypeStruct((OCC, VIRT, LANES),...]
where the time goes in v5:
time: 45 us; the launch traced here: 44.8 us
  Pallas kernels  43.9 us (98%)
  local copies, waits for them, and re-layouts  0.95 us (2%)
    pallas_call x1, Pallas kernels, local_block(): pl.pallas_call(kernel, out_shape=jax.ShapeDtypeStruct((OCC, VIRT, LANES),...  43.9 us
    unnamed x1, local copies, waits for them, and re-layouts  0.95 us

profile of v5, /device:TPU:0, one launch (start us, length us, event | category | flops | bytes accessed | tf_op | source)
XLA Modules:
  0.0 44.8 jit_solution(12320026642437203763)
XLA Ops:
  0.0 43.9 %shard_map.37 = f32[24,80,120]{2,1,0:T(8,128)S(1)} custom-call(bf16[32,32,128,128]{3,2,1,0:T(8,128)(2,1)} %ao_ref.1, bf16[24,128]{1,0:T(8,128)(2,1)} %bitcast.3, bf16[80,128]{1,0:T(8,128)(2,1)} %bitcast.2), custom_call_target="tpu_custom_call" | custom-call | tf_op jit(solution)/shard_map/pallas_call | solution.py:343
  43.9 0.9 %copy.5 = f32[24,80,120]{2,1,0:T(8,128)} copy(f32[24,80,120]{2,1,0:T(8,128)S(1)} %shard_map.37) | data formatting | bytes 1843200

commit v6 on v5

--- a/solution.py
+++ b/solution.py
@@ -18,9 +18,9 @@
 RIDERS = KEPT // SPECIAL
 FREE = 128 - LANES
 PART = 32 * OCC
-STEPS = 17
-LATE = 9
-SLOTS = 16
+STEPS = 16
+HALF = 8
+SLOTS = 8
 AHEAD = 6
 QGRP = 8
 GROUPS = 4
@@ -28,14 +28,15 @@
 Y_RING = 8
 OWN = ((0, 8), (8, 8), (16, 8), (24, 6))
 NEAR = ((0, 4), (4, 4), (8, 8), (16, 8), (24, 6))
-SWITCH = 4
+SWITCH = 3
 CROSS_SUM = 3
 CROSS_SUM_2 = 4
-NEAR_AT = (7, 8, 11, 15, 17)
-NEAR_SUM = (11, 12, 15, 19, 21)
-OWN_AT = (17, 17, 18, 19)
-V_AT = (21, 22, 23)
-END = 24
+NEAR_AT = (10, 12, 13, 15, 16)
+NEAR_SUM = (14, 14, 17, 19, 20)
+OWN_AT = (16, 16, 17, 18)
+V_AT = (20, 21, 22)
+END = 23
+CROSS_Q = (7, 9, 8, 6)
 
 
 def dot(a, b):
@@ -55,9 +56,9 @@
 
 
 def kernel(ao_ref, occ_hbm, virt_hbm, out_ref,
-           a_buf, a_late, occ_lhs, virt_rhs, kron_own, kron_sib, virt_v,
+           a_buf, occ_lhs, virt_rhs, kron_own, kron_sib, virt_v,
            h_buf, h_in, e_special, e_buf, y_in, e_all, occ_ref, virt_ref,
-           c_sem, a_sem, al_sem, hs_sem, hr_sem, hl_sem, ys_sem, yc_sem, yn_sem, yo_sem,
+           c_sem, a_sem, hs_sem, hr_sem, ys_sem, yc_sem, yn_sem, yo_sem,
            zs_sem, zc_sem, zn_sem):
     z = lax.axis_index("dev2")
     dev = lax.axis_index("dev")
@@ -77,16 +78,29 @@
             q = q * OCC
         return pl.ds(q, n * OCC)
 
-    def a_copy(q, n, s):
-        return pltpu.make_async_copy(
-            ao_ref.at[:, pl.ds(q, n)], a_buf.at[:, pl.ds(q % SLOTS, n)], a_sem.at[s % 8])
-
-    a_copy_late = pltpu.make_async_copy(ao_ref.at[:, 31], a_late, al_sem)
-
-    def h_copy(q, n, sem):
+    def first_q(s):
+        if isinstance(s, int):
+            return s // HALF * RIDERS + max(2 * (s % HALF) - 1, 0)
+        return s // HALF * RIDERS + jnp.maximum(2 * (s % HALF) - 1, 0)
+
+    def a_start(s):
+        special = s % HALF == 0
+        q = first_q(s)
+        for k in range(2):
+            if isinstance(s, int):
+                at = (KEPT + s // HALF if k == 0 else q) if special else q + k
+            else:
+                at = jnp.where(special, (q, KEPT + s // HALF)[1 - k], q + k)
+            pltpu.make_async_copy(ao_ref.at[:, at], a_buf.at[s % SLOTS, :, k], a_sem.at[s % SLOTS]).start()
+
+    def a_wait(s):
+        pltpu.make_async_copy(ao_ref.at[:, pl.ds(0, 2)], a_buf.at[s % SLOTS], a_sem.at[s % SLOTS]).wait()
+
+    def h_copy(s):
+        rows = pl.ds(s * 2, 2)
         return pltpu.make_async_remote_copy(
-            src_ref=h_buf.at[1 - core, pl.ds(q, n)], dst_ref=h_in.at[pl.ds(q, n)],
-            send_sem=hs_sem, recv_sem=sem,
+            src_ref=h_buf.at[1 - core, rows], dst_ref=h_in.at[rows],
+            send_sem=hs_sem, recv_sem=hr_sem.at[s % H_RING],
             device_id={"dev": sib}, device_id_type=MESH)
 
     def y_copy(z0, zn, q, n, sem):
@@ -122,19 +136,13 @@
     def when_step(s, first, end, shift, do):
         t = s - shift
 
-        if first == 0:
-            @pl.when(t == 0)
-            def _():
-                do(30, 1, 0)
-
-        if first < 3:
-            @pl.when((t == 1) | (t == 2))
-            def _():
-                do(t - 1, 1, t)
-
-        @pl.when((t >= max(first, 3)) & (t < end))
+        @pl.when((t >= first) & (t < end) & (t % HALF == 0))
         def _():
-            do(2 * t - 4, 2, t)
+            do(t // HALF * RIDERS, 1, t)
+
+        @pl.when((t >= first) & (t < end) & (t % HALF != 0))
+        def _():
+            do(first_q(t), 2, t)
 
     barrier = pltpu.get_barrier_semaphore()
     for peer in ({"dev": sib}, {"dev": across}, {"dev2": (z + 1) % 4}, {"dev2": (z + 2) % 4}, {"dev2": (z + 3) % 4}):
@@ -144,13 +152,13 @@
                 pltpu.make_async_copy(virt_hbm, virt_ref, c_sem.at[1]))
     for c in c_copies:
         c.start()
-    a_copy(30, 1, 0).start()
+    a_start(0)
     for i in range(OCC):
         out_ref[i] = jnp.zeros((VIRT, LANES), F32)
     for c in c_copies:
         c.wait()
     for s in range(1, AHEAD):
-        a_copy(*((s - 1, 1) if s < 3 else (2 * s - 4, 2)), s).start()
+        a_start(s)
 
     row = iota((OCC, OCC), 0)
     perm = select(iota((OCC, OCC), 1) == 3 * (row % 8) + row // 8)
@@ -177,11 +185,11 @@
         pick_q = select(iota((128, 96), 0) == (col % 32) // QGRP * 32 + g * QGRP + col % QGRP)
         virt_v[g] = dot(virt_ref[...], pick_q).astype(BF16)
 
-    def half_step(tiles, q, n):
+    def half_step(s):
         rows = []
-        for qq in range(n):
+        for qq in range(2):
             for p in range(0, 32, 4):
-                a = [tiles(p + k, qq) for k in range(4)]
+                a = [a_buf[s % SLOTS, p + k, qq] for k in range(4)]
                 w = jnp.concatenate(
                     [jnp.concatenate(a[:2], 1), jnp.concatenate(a[2:], 1)], 0)
                 r = dot(occ_lhs[...], w)
@@ -190,22 +198,28 @@
                     rows.append(jnp.concatenate([part[0:8], part[8:16], part[16:24]], 1))
         t_one = jnp.concatenate(rows, 0).astype(BF16)
         h = dot(t_one, virt_rhs[...]).astype(BF16)
-        for qq in range(n):
-            h_buf[0, q + qq] = h[qq * 256:(qq + 1) * 256, :128]
-            h_buf[1, q + qq] = h[qq * 256:(qq + 1) * 256, 128:]
-
-    def contract_p(q, n):
-        own = jnp.concatenate([h_buf[core, q + k] for k in range(n)], 1)
-        other = jnp.concatenate([h_in[q + k] for k in range(n)], 1)
+        for qq in range(2):
+            h_buf[0, s * 2 + qq] = h[qq * 256:(qq + 1) * 256, :128]
+            h_buf[1, s * 2 + qq] = h[qq * 256:(qq + 1) * 256, 128:]
+
+    def contract_p(s):
+        own = jnp.concatenate([h_buf[core, s * 2 + k] for k in range(2)], 1)
+        other = jnp.concatenate([h_in[s * 2 + k] for k in range(2)], 1)
         return dot(kron_own[...], own) + dot(kron_sib[...], other)
 
-    def e_step(q, n):
-        e = contract_p(q, n)
+    def e_step(q, n, s):
+        e = contract_p(s)
         free = iota((192, 128), 1) >= LANES
+        g = s // HALF
+        if n == 1:
+            e_special[g] = e[:, :128]
         for k in range(n):
-            at = (q + k) % RIDERS * FREE
-            rider = pltpu.roll(e_special[(q + k) // RIDERS], LANES - at, 1)
-            row = jnp.where(free, rider, e[:, k * 128:(k + 1) * 128])
+            if n == 1:
+                rider = pltpu.roll(e[:, :128], LANES, 1)
+            else:
+                rider = pltpu.roll(e_special[g], LANES - (q + k) % RIDERS * FREE, 1)
+            k_at = k + 2 - n
+            row = jnp.where(free, rider, e[:, k_at * 128:(k_at + 1) * 128])
             for yy in range(2):
                 for zz in range(4):
                     r = (yy * 4 + zz) * OCC
@@ -244,7 +258,8 @@
         rows = rows_of(q, n)
         e_all[rows_of(z * 32 + q, n)] = e_buf[y, z, rows] + y_in[z, rows]
         z_wait(n, zn_sem.at[g])
-        z_wait(2 * n, zc_sem.at[g])
+        for k in ((0, 1), (), (2,), (3,))[g]:
+            z_wait(2 * CROSS_Q[k], zc_sem.at[k])
         if g == 1:
             unpack(0, 0, 15)
         if g == 2:
@@ -254,42 +269,24 @@
         v_group(g)
 
     def step(s, carry):
-        def transform(q, n, t):
-            a_copy(q, n, t).wait()
-
-            @pl.when(t + AHEAD < STEPS)
-            def _():
-                a_copy(2 * (t + AHEAD) - 4, 2, t + AHEAD).start()
-            slot = q % SLOTS
-            half_step(lambda p, qq: a_buf[p, slot + qq], q, n)
-            if isinstance(q, int):
+        @pl.when(s < STEPS)
+        def _():
+            a_wait(s)
+
+            @pl.when(s + AHEAD < STEPS)
+            def _():
+                a_start(s + AHEAD)
+            half_step(s)
+
+            @pl.when(s == 0)
+            def _():
                 pl.semaphore_wait(barrier, 5)
-            h_copy(q, n, hr_sem.at[t % H_RING]).start()
-
-        when_step(s, 0, STEPS, 0, transform)
-
-        @pl.when(s == 2)
-        def _():
-            a_copy_late.start()
-
-        @pl.when(s == LATE)
-        def _():
-            a_copy_late.wait()
-            half_step(lambda p, qq: a_late[p], 31, 1)
-            h_copy(31, 1, hl_sem).start()
-
-        @pl.when(s == LATE + 1)
-        def _():
-            h_copy(31, 1, hl_sem).wait_recv()
-            e_special[1] = contract_p(31, 1)
+            h_copy(s).start()
 
         def to_e(q, n, t):
-            h_copy(q, n, hr_sem.at[t % H_RING]).wait_recv()
-            if isinstance(q, int):
-                e_special[0] = contract_p(30, 1)
-            else:
-                e_step(q, n)
-                y_cross(q, n, t).start()
+            h_copy(t).wait_recv()
+            e_step(q, n, t)
+            y_cross(q, n, t).start()
 
         when_step(s, 0, STEPS, 1, to_e)
 
@@ -305,10 +302,10 @@
 
         def to_z(q, n, t):
             y_cross(q, n, t).wait_recv()
-            add_send(far, q, n, zc_sem.at[q // QGRP])
-            add_send(far_near, q, n, zc_sem.at[q // QGRP])
-
-        when_step(s, 1, SWITCH, CROSS_SUM, to_z)
+            add_send(far, q, n, zc_sem.at[(q + n - 1) // QGRP])
+            add_send(far_near, q, n, zc_sem.at[(q + n - 1) // QGRP])
+
+        when_step(s, 0, SWITCH, CROSS_SUM, to_z)
         when_step(s, SWITCH, STEPS, CROSS_SUM_2, to_z)
 
         for k in range(len(NEAR)):
@@ -327,7 +324,7 @@
     finish(GROUPS - 1)
 
     pltpu.make_async_remote_copy(
-        src_ref=h_buf.at[1 - core], dst_ref=h_in, send_sem=hs_sem, recv_sem=hl_sem,
+        src_ref=h_buf.at[1 - core], dst_ref=h_in, send_sem=hs_sem, recv_sem=hr_sem.at[0],
         device_id={"dev": sib}, device_id_type=MESH).wait_send()
     y_copy(0, 4, 0, KEPT, yo_sem.at[0]).wait_send()
     rows = pl.ds(0, 3 * KEPT * OCC)
@@ -346,8 +343,7 @@
             in_specs=[hbm, hbm, hbm],
             out_specs=pl.BlockSpec(memory_space=pltpu.VMEM),
             scratch_shapes=[
-                pltpu.VMEM((32, SLOTS, 128, 128), BF16),
-                pltpu.VMEM((32, 128, 128), BF16),
+                pltpu.VMEM((SLOTS, 32, 2, 128, 128), BF16),
                 pltpu.VMEM((2 * OCC, 256), BF16),
                 pltpu.VMEM((384, 256), BF16),
                 pltpu.VMEM((192, 256), BF16),
@@ -361,8 +357,8 @@
                 pltpu.VMEM((4 * PART, 128), F32),
                 pltpu.VMEM((OCC, 128), BF16),
                 pltpu.VMEM((VIRT, 128), BF16),
-                dma((2,)), dma((8,)), dma,
-                dma, dma((H_RING,)), dma,
+                dma((2,)), dma((SLOTS,)),
+                dma, dma((H_RING,)),
                 dma, dma((Y_RING,)), dma((len(NEAR),)), dma((GROUPS,)),
                 dma, dma((GROUPS,)), dma((GROUPS,)),
             ],

time: 45 us -> 44.7 us (level)
  no operation moved by 1% of the time
where the time goes in v6:
time: 44.7 us; the launch traced here: 44.5 us
  Pallas kernels  43.6 us (98%)
  local copies, waits for them, and re-layouts  0.95 us (2%)
    pallas_call x1, Pallas kernels, local_block(): pl.pallas_call(kernel, out_shape=jax.ShapeDtypeStruct((OCC, VIRT, LANES),...  43.6 us
    unnamed x1, local copies, waits for them, and re-layouts  0.95 us

profile of v6, /device:TPU:0, one launch (start us, length us, event | category | flops | bytes accessed | tf_op | source)
XLA Modules:
  0.0 44.5 jit_solution(6962546244455050017)
XLA Ops:
  0.0 43.6 %shard_map.37 = f32[24,80,120]{2,1,0:T(8,128)S(1)} custom-call(bf16[32,32,128,128]{3,2,1,0:T(8,128)(2,1)} %ao_ref.1, bf16[24,128]{1,0:T(8,128)(2,1)} %bitcast.3, bf16[80,128]{1,0:T(8,128)(2,1)} %bitcast.2), custom_call_target="tpu_custom_call" | custom-call | tf_op jit(solution)/shard_map/pallas_call | solution.py:340
  43.6 0.9 %copy.5 = f32[24,80,120]{2,1,0:T(8,128)} copy(f32[24,80,120]{2,1,0:T(8,128)S(1)} %shard_map.37) | data formatting | bytes 1843200

commit v7 on v6

--- a/solution.py
+++ b/solution.py
@@ -27,12 +27,12 @@
 H_RING = 4
 Y_RING = 8
 OWN = ((0, 8), (8, 8), (16, 8), (24, 6))
-NEAR = ((0, 4), (4, 4), (8, 8), (16, 8), (24, 6))
+NEAR = ((0, 8), (8, 8), (16, 8), (24, 6))
 SWITCH = 3
 CROSS_SUM = 3
 CROSS_SUM_2 = 4
-NEAR_AT = (10, 12, 13, 15, 16)
-NEAR_SUM = (14, 14, 17, 19, 20)
+NEAR_AT = (11, 13, 15, 16)
+NEAR_SUM = (14, 17, 19, 20)
 OWN_AT = (16, 16, 17, 18)
 V_AT = (20, 21, 22)
 END = 23

time: 44.7 us -> 45 us (level)
  no operation moved by 1% of the time
where the time goes in v7:
time: 45 us; the launch traced here: 44.8 us
  Pallas kernels  43.9 us (98%)
  local copies, waits for them, and re-layouts  0.95 us (2%)
    pallas_call x1, Pallas kernels, local_block(): pl.pallas_call(kernel, out_shape=jax.ShapeDtypeStruct((OCC, VIRT, LANES),...  43.9 us
    unnamed x1, local copies, waits for them, and re-layouts  0.95 us

profile of v7, /device:TPU:0, one launch (start us, length us, event | category | flops | bytes accessed | tf_op | source)
XLA Modules:
  0.0 44.8 jit_solution(15011761380112620236)
XLA Ops:
  0.0 43.9 %shard_map.37 = f32[24,80,120]{2,1,0:T(8,128)S(1)} custom-call(bf16[32,32,128,128]{3,2,1,0:T(8,128)(2,1)} %ao_ref.1, bf16[24,128]{1,0:T(8,128)(2,1)} %bitcast.3, bf16[80,128]{1,0:T(8,128)(2,1)} %bitcast.2), custom_call_target="tpu_custom_call" | custom-call | tf_op jit(solution)/shard_map/pallas_call | solution.py:340
  43.9 0.9 %copy.5 = f32[24,80,120]{2,1,0:T(8,128)} copy(f32[24,80,120]{2,1,0:T(8,128)S(1)} %shard_map.37) | data formatting | bytes 1843200
